TPU v7x, 32 devices: a whole 2x2x4 slice. The times are simulated.
32 devices in a mesh: region: 2 (over x), blk: 16 (over z, y, core).
Axes of the slice: x: 2, y: 2, z: 4, core: 2. Of those that a mesh axis runs over, the one named last changes fastest.
Arguments:
- ensemble: float32 [64, 256, 128], P(('region', 'blk'))
- observed: float32 [64, 256, 128], P(('region', 'blk')), may hold values from -6 to 6
- obs_var: float32 [64, 256], P(('region', 'blk')), may hold values from 0.5 to 2
- ridge: float32 [64], P(('region', 'blk')), may hold values from 0.05 to 0.5
- pred_back: int32 [64, 12], P(('region', 'blk')), may hold values from 0 to 16, as said below
- bounds: float32 [2], replicated, may hold values from 0.2 to 6, as said below
Outputs:
- analysis: float32 [64, 256, 128], P(('region', 'blk'))
Inputs may be any that keep to these rules, and one draw needn't show every extreme that they name: `pred_back`: each row holds distinct distances among 1 to 16, never more than the block's own index, with 0 for an empty slot; the last block fills all 12 slots. bounds[0] < bounds[1].
All inputs are finite; a program needn't handle non-finite values.
Results may differ from a plain program's by a relative error of at most 0.0003.
Values sent between devices are 32-bit elements; how exact they have to be, the bound alone decides.
A program may use at most 192 MiB of HBM per device.

v0:
```python
import functools
import math

import jax
import jax.numpy as jnp
from jax import lax
from jax.experimental import pallas as pl
from jax.experimental.pallas import tpu as pltpu
from jax.sharding import PartitionSpec as P

REACH = 16
ITERS = 3


def from_behind(value, axis, steps):
    count = lax.axis_size(axis)
    first, last = (max(0, -steps), min(count, count - steps))
    return lax.ppermute(value, axis, [(source, source + steps) for source in range(first, last)])


def small_solve(gram, target):
    size = gram.shape[0]
    factor = {}
    for block_position in range(size):
        running = gram[block_position, block_position]
        for k in range(block_position):
            running = running - factor[block_position, k] * factor[block_position, k]
        factor[block_position, block_position] = jnp.sqrt(running)
        for i in range(block_position + 1, size):
            running = gram[i, block_position]
            for k in range(block_position):
                running = running - factor[i, k] * factor[block_position, k]
            factor[i, block_position] = running / factor[block_position, block_position]
    forward = []
    for i in range(size):
        running = target[i]
        for k in range(i):
            running = running - factor[i, k] * forward[k]
        forward.append(running / factor[i, i])
    analysis_output = [None] * size
    for i in reversed(range(size)):
        running = forward[i]
        for k in range(i + 1, size):
            running = running - factor[k, i] * analysis_output[k]
        analysis_output[i] = running / factor[i, i]
    return jnp.stack(analysis_output)


def previous_blocks(entry_values, reach_devices):
    pieces = [
        from_behind(entry_values, ("region", "blk"), shift_by)
        for shift_by in range(reach_devices, 0, -1)
    ]
    return jnp.concatenate(pieces, axis=0)


def on_device(ensemble, observed, obs_var, ridge, pred_back, bounds):
    highest = lax.Precision.HIGHEST
    local_blocks, rows, members = ensemble.shape
    slots = pred_back.shape[1]
    reach_devices = -(-REACH // local_blocks)
    before = reach_devices * local_blocks
    anomaly = (ensemble - jnp.mean(ensemble, axis=2, keepdims=True)) / jnp.sqrt(
        jnp.float32(members - 1)
    )
    positions = before + jnp.arange(local_blocks, dtype=jnp.int32)[:, None] - pred_back
    positions = jnp.where(pred_back > 0, positions, before + local_blocks)
    empty_zero_matrix = jnp.zeros((1, rows, members), jnp.float32)

    def extend(entry_values):
        return jnp.concatenate(
            [previous_blocks(entry_values, reach_devices), entry_values, empty_zero_matrix], axis=0
        )

    preds = extend(anomaly)[positions]
    identity = jnp.eye(slots, dtype=jnp.float32)
    gram = jnp.einsum("bjrm,bkrm->jkbr", preds, preds, precision=highest)
    gram = gram + ridge[None, None, :, None] * identity[:, :, None, None]
    target = jnp.einsum("bjrm,brm->jbr", preds, anomaly, precision=highest)
    regression_coefficients = small_solve(gram, target)
    resid = anomaly - jnp.einsum("jbr,bjrm->brm", regression_coefficients, preds, precision=highest)
    inverse_var = 1.0 / (jnp.sum(resid * resid, axis=2) + 1e-05)
    inverse_obs = 1.0 / obs_var
    beta_blocks = jnp.transpose(regression_coefficients, (1, 0, 2))
    lower_bound = bounds[0]
    upper_bound = bounds[1]
    theta = (upper_bound + lower_bound) / 2
    delta = (upper_bound - lower_bound) / 2
    sigma = theta / delta
    rho_now = 1.0 / sigma
    residue = inverse_obs[:, :, None] * (observed - ensemble)
    increment = jnp.zeros_like(ensemble)
    direction = residue / theta
    for step in range(ITERS):
        increment = increment + direction
        extended = extend(direction)
        lower_analysis_output = direction
        for lower_slot in range(slots):
            lower_analysis_output = (
                lower_analysis_output
                - beta_blocks[:, lower_slot, :, None] * extended[positions[:, lower_slot]]
            )
        upper_entry_values = lower_analysis_output * inverse_var[:, :, None]
        window = jnp.zeros((before + local_blocks + 1, rows, members), jnp.float32)
        for slot in range(slots):
            window = window.at[positions[:, slot]].add(
                beta_blocks[:, slot, :, None] * upper_entry_values
            )
        analysis_output = upper_entry_values - window[before : before + local_blocks]
        for shift_by in range(1, reach_devices + 1):
            start = (reach_devices - shift_by) * local_blocks
            analysis_output = analysis_output - from_behind(
                window[start : start + local_blocks], ("region", "blk"), -shift_by
            )
        residue = residue - (analysis_output + inverse_obs[:, :, None] * direction)
        rho_next = 1.0 / (2 * sigma - rho_now)
        direction = rho_next * rho_now * direction + 2 * rho_next / delta * residue
        rho_now = rho_next
    increment = increment + direction
    return ensemble + increment


VMEM_GRANT = 66_700_000
SUB = 8
LANES = 128
MESH_ID = pl.DeviceIdType.MESH


def place():
    per = lax.axis_size("blk")
    me = lax.axis_index("region") * per + lax.axis_index("blk")
    return per, me


def greet(n, per, me):
    barrier = pltpu.get_barrier_semaphore()

    def signal(i, carry):
        k = lax.rem(me + i, n)
        pl.semaphore_signal(
            barrier, inc=1, device_id=(k // per, lax.rem(k, per)), device_id_type=MESH_ID
        )
        return carry

    lax.fori_loop(1, n, signal, 0)
    pl.semaphore_wait(barrier, n - 1)


def copy_to(src, dst, send_sem, recv_sem, k, per):
    return pltpu.make_async_remote_copy(
        src_ref=src,
        dst_ref=dst,
        send_sem=send_sem,
        recv_sem=recv_sem,
        device_id=(k // per, lax.rem(k, per)),
        device_id_type=MESH_ID,
    )


def gather_rows(n, per, me, loads, ens, obs, obs_var, ridge, pred_back, pack, ens_r, obs_r, pack_r, sems):
    send_sem, recv_sem = sems
    local, rows, members = ens.shape
    mine = pl.ds(me * local, local)

    def send_ens(i, carry):
        k = lax.rem(me + i, n)
        part = pl.ds(pl.multiple_of(k * SUB, SUB), SUB)
        copy_to(ens.at[:, part, :], ens_r.at[mine], send_sem.at[0], recv_sem.at[0], k, per).start()
        return carry

    loads[0].wait()
    lax.fori_loop(1, n, send_ens, 0)
    for load in loads[1:]:
        load.wait()

    lane = lax.broadcasted_iota(jnp.int32, (1, LANES), 1)
    groups = LANES // SUB
    for block in range(local):
        meta = jnp.where(lane == SUB + REACH, ridge[block], 0.0)
        for slot in range(pred_back.shape[1]):
            back = pred_back[block, slot]
            meta = jnp.where((lane == back + (SUB - 1)) & (lane >= SUB), 1.0, meta)
        for half in range(rows // LANES):
            row = obs_var[block : block + 1, half * LANES : (half + 1) * LANES]
            for k in range(groups):
                turned = row if k == 0 else pltpu.roll(row, LANES - SUB * k, 1)
                pack[half * groups + k, block] = jnp.where(lane < SUB, turned, meta)

    def send_pack(i, carry):
        k = lax.rem(me + i, n)
        copy_to(pack.at[k], pack_r.at[mine], send_sem.at[1], recv_sem.at[1], k, per).start()
        return carry

    lax.fori_loop(1, n, send_pack, 0)

    def send_obs(i, carry):
        k = lax.rem(me + i, n)
        part = pl.ds(pl.multiple_of(k * SUB, SUB), SUB)
        copy_to(obs.at[:, part, :], obs_r.at[mine], send_sem.at[2], recv_sem.at[2], k, per).start()
        return carry

    lax.fori_loop(1, n, send_obs, 0)
    own = pl.ds(pl.multiple_of(me * SUB, SUB), SUB)
    ens_r[mine] = ens[:, own, :]
    obs_r[mine] = obs[:, own, :]
    pack_r[mine] = pack[me]


def whole_kernel(
    n, bounds_in, ens_in, obs_in, obs_var_in, ridge_in, pred_back_in, z,
    bounds, ens, obs, obs_var, ridge, pred_back, load_sem, pack, ens_r, obs_r, pack_r, z_r, send_sem, recv_sem,
    apad, dpad, upad, res, ivar, iobs, corr, wide,
):
    per, me = place()
    local = ens.shape[0]
    loads = [
        pltpu.make_async_copy(src, dst, load_sem.at[i])
        for i, (src, dst) in enumerate(
            (
                (ens_in, ens),
                (obs_in, obs),
                (obs_var_in, obs_var),
                (ridge_in, ridge),
                (pred_back_in, pred_back),
                (bounds_in, bounds),
            )
        )
    ]
    for load in loads:
        load.start()
    greet(n, per, me)
    gather_rows(
        n, per, me, loads, ens, obs, obs_var, ridge, pred_back, pack, ens_r, obs_r, pack_r,
        (send_sem, recv_sem),
    )
    other = lax.rem(me + 1, n)
    sent = pl.ds(0, (n - 1) * SUB)
    got = pl.ds(0, (n - 1) * local)
    whole = (
        (ens.at[:, sent, :], ens_r.at[got]),
        (pack.at[pl.ds(0, n - 1)], pack_r.at[got]),
        (obs.at[:, sent, :], obs_r.at[got]),
        (z_r.at[got], z.at[:, sent, :]),
    )

    def arrived(which):
        ref = whole[which][1]
        copy_to(ref, ref, send_sem.at[which], recv_sem.at[which], other, per).wait_recv()

    rows_part(
        n * local, arrived, bounds, ens_r, obs_r, pack_r, z_r,
        apad, dpad, upad, res, ivar, iobs, corr, wide,
    )
    own = pl.ds(pl.multiple_of(me * SUB, SUB), SUB)

    def send(i, carry):
        k = lax.rem(me + i, n)
        copy_to(
            z_r.at[pl.ds(k * local, local)], z.at[:, own, :], send_sem.at[3], recv_sem.at[3], k, per
        ).start()
        return carry

    lax.fori_loop(1, n, send, 0)
    z[:, own, :] = z_r[pl.ds(me * local, local)]
    arrived(3)
    for which, (ref, unused) in enumerate(whole):
        copy_to(ref, ref, send_sem.at[which], recv_sem.at[which], other, per).wait_send()


def rows_part(nb, arrived, bounds, ens, obs, pack, z, apad, dpad, upad, res, ivar, iobs, corr, wide):
    members = ens.shape[2]
    tile = (SUB, LANES)
    zero = jnp.zeros(tile, jnp.float32)
    for i in range(REACH):
        apad[i] = zero
        dpad[i] = zero
        upad[nb + i] = zero
    arrived(0)
    x = ens[...]
    mean = jnp.sum(x, axis=2, keepdims=True) * (1.0 / members)
    apad[pl.ds(REACH, nb)] = (x - mean) * (1.0 / math.sqrt(members - 1))

    lane = lax.broadcasted_iota(jnp.int32, (nb, LANES), 1)
    back = lane - lax.broadcasted_iota(jnp.int32, (nb, LANES), 0)
    for r in range(SUB):
        lhs = apad[pl.ds(REACH, nb), r, :]
        rhs = jnp.concatenate([lhs, jnp.zeros((LANES - nb, members), jnp.float32)], axis=0)
        full = lax.dot_general(
            lhs,
            rhs,
            (((1,), (1,)), ((), ())),
            precision=lax.Precision.HIGHEST,
            preferred_element_type=jnp.float32,
        )
        for delta in range(REACH + 1):
            corr[delta, r : r + 1, :] = jnp.sum(
                jnp.where(back == delta, full, 0.0), axis=0, keepdims=True
            )

    arrived(1)
    flat = pack[...].reshape(nb, LANES)
    turned = jnp.concatenate([flat, jnp.zeros((LANES - nb, LANES), jnp.float32)], axis=0).T
    obs_rows = turned[0:SUB]
    on_lane = lax.broadcasted_iota(jnp.int32, tile, 1)
    chosen = [
        jnp.broadcast_to(turned[SUB + d : SUB + d + 1], tile) > 0.5 for d in range(REACH)
    ]
    at = SUB + REACH
    ridge = jnp.where(on_lane < nb, jnp.broadcast_to(turned[at : at + 1], tile), 1.0)

    factor = {}
    inverse = []
    for j in range(REACH):
        for i in range(j, REACH):
            value = pltpu.roll(corr[i - j], j + 1, 1)
            running = jnp.where(chosen[j], jnp.where(chosen[i], value, 0.0), 0.0)
            if i == j:
                running = running + ridge
            for k in range(j):
                running = running - factor[i, k] * factor[j, k]
            if i == j:
                inverse.append(1.0 / jnp.sqrt(running))
            else:
                factor[i, j] = running * inverse[j]
    forward = []
    for i in range(REACH):
        running = jnp.where(chosen[i], corr[i + 1], 0.0)
        for k in range(i):
            running = running - factor[i, k] * forward[k]
        forward.append(running * inverse[i])
    beta = [None] * REACH
    for i in reversed(range(REACH)):
        running = forward[i]
        for k in range(i + 1, REACH):
            running = running - factor[k, i] * beta[k]
        beta[i] = running * inverse[i]
    for d in range(REACH):
        for g in range(nb + REACH):
            wide[g, d] = jnp.broadcast_to(beta[d][:, g : g + 1], tile) if g < nb else zero
    inverse_obs = 1.0 / jnp.where(on_lane < nb, obs_rows, 1.0)
    for g in range(nb):
        iobs[g] = jnp.broadcast_to(inverse_obs[:, g : g + 1], tile)

    def lower(ref, g0):
        values = [ref[g0 + i] for i in range(REACH + SUB)]
        outs = []
        for g in range(SUB):
            total = values[REACH + g]
            for d in range(REACH):
                total = total - wide[g0 + g, d] * values[REACH + g - d - 1]
            outs.append(total)
        return outs

    def upper(ref, g0):
        values = [ref[g0 + i] for i in range(REACH + SUB)]
        outs = []
        for g in range(SUB):
            total = values[g]
            for d in range(REACH):
                total = total - wide[g0 + g + d + 1, d] * values[g + d + 1]
            outs.append(total)
        return outs

    arrived(2)
    lo = jnp.full(tile, bounds[0], jnp.float32)
    hi = jnp.full(tile, bounds[1], jnp.float32)
    theta = (hi + lo) / 2
    delta = (hi - lo) / 2
    sigma = theta / delta
    rho = 1.0 / sigma

    def start(t, carry):
        g0 = t * SUB
        for g, resid in enumerate(lower(apad, g0)):
            total = jnp.sum(resid * resid, axis=1, keepdims=True) + 1e-05
            ivar[g0 + g] = jnp.broadcast_to(1.0 / total, tile)
            rhs = iobs[g0 + g] * (obs[g0 + g] - ens[g0 + g])
            res[g0 + g] = rhs
            first = rhs / theta
            dpad[REACH + g0 + g] = first
            z[g0 + g] = first
        return carry

    lax.fori_loop(0, nb // SUB, start, 0)
    for step in range(ITERS):
        rho_next = 1.0 / (2 * sigma - rho)
        keep = rho_next * rho
        move = 2 * rho_next / delta
        rho = rho_next

        def down(t, carry):
            g0 = t * SUB
            for g, value in enumerate(lower(dpad, g0)):
                upad[g0 + g] = value * ivar[g0 + g]
            return carry

        def up(t, carry):
            g0 = t * SUB
            for g, value in enumerate(upper(upad, g0)):
                old = dpad[REACH + g0 + g]
                left = res[g0 + g] - (value + iobs[g0 + g] * old)
                fresh = keep * old + move * left
                res[g0 + g] = left
                dpad[REACH + g0 + g] = fresh
                z[g0 + g] = z[g0 + g] + fresh
            return carry

        lax.fori_loop(0, nb // SUB, down, 0)
        lax.fori_loop(0, nb // SUB, up, 0)


def by_rows(n, ensemble, observed, obs_var, ridge, pred_back, bounds):
    local, rows, members = ensemble.shape
    nb = n * local
    f32 = jnp.float32
    vmem = pl.BlockSpec(memory_space=pltpu.VMEM)
    hbm = pl.BlockSpec(memory_space=pltpu.HBM)
    blocks = lambda count: pltpu.VMEM((count, SUB, members), f32)
    z = pl.pallas_call(
        functools.partial(whole_kernel, n),
        out_shape=jax.ShapeDtypeStruct(ensemble.shape, f32),
        in_specs=[hbm] * 6,
        out_specs=vmem,
        scratch_shapes=[
            pltpu.SMEM(bounds.shape, f32),
            pltpu.VMEM(ensemble.shape, f32),
            pltpu.VMEM(observed.shape, f32),
            pltpu.VMEM(obs_var.shape, f32),
            pltpu.SMEM(ridge.shape, f32),
            pltpu.SMEM(pred_back.shape, jnp.int32),
            pltpu.SemaphoreType.DMA((6,)),
            pltpu.VMEM((n, local, 1, LANES), f32),
            blocks(nb),
            blocks(nb),
            pltpu.VMEM((nb, 1, LANES), f32),
            blocks(nb),
            pltpu.SemaphoreType.DMA((4,)),
            pltpu.SemaphoreType.DMA((4,)),
            blocks(nb + REACH),
            blocks(nb + REACH),
            blocks(nb + REACH),
            blocks(nb),
            blocks(nb),
            blocks(nb),
            pltpu.VMEM((REACH + 1, SUB, LANES), f32),
            pltpu.VMEM((nb + REACH, REACH, SUB, LANES), f32),
        ],
        compiler_params=pltpu.CompilerParams(
            collective_id=0, has_side_effects=True, vmem_limit_bytes=VMEM_GRANT
        ),
        name="whole",
    )(bounds, ensemble, observed, obs_var, ridge, pred_back)
    return ensemble + z


def choose(n, ensemble, *rest):
    local, rows, members = ensemble.shape
    fits = rows == n * SUB and members == LANES and n * local + REACH <= LANES
    if fits and (n * local) % SUB == 0:
        return by_rows(n, ensemble, *rest)
    return on_device(ensemble, *rest)


def solution(mesh):
    return jax.shard_map(
        functools.partial(choose, mesh.size),
        mesh=mesh,
        in_specs=(
            P(("region", "blk"), None, None),
            P(("region", "blk"), None, None),
            P(("region", "blk"), None),
            P(("region", "blk")),
            P(("region", "blk"), None),
            P(),
        ),
        out_specs=P(("region", "blk"), None, None),
        check_vma=False,
    )
```

profile of v0, /device:TPU:0, one launch (start us, length us, event | category | flops | bytes accessed | tf_op | source)
XLA Modules:
  0.0 35.1 jit_solution(3792961349721396956)
XLA Ops:
  0.0 0.0 copy-start
  0.0 33.4 %whole.1 = f32[2,256,128]{2,1,0:T(8,128)} custom-call(f32[2]{0:T(128)} %bounds_in.1, f32[2,256,128]{2,1,0:T(8,128)} %ens_in.1, f32[2,256,128]{2,1,0:T(8,128)} %obs_in.1, f32[2,256]{1,0:T(2,128)} %obs_var_in.1, f32[2]{0:T(128)} %ridge_in.1, s32[2,12]{1,0:T(2,128)} %pred_back_in.1), custom_call_target="tpu_custom_call" | custom-call | tf_op jit(solution)/shard_map/whole/pallas_call | solution.py:419
  33.4 0.0 copy-done
  33.4 1.7 %add.3 = f32[2,256,128]{2,1,0:T(8,128)} add(f32[2,256,128]{2,1,0:T(8,128)S(1)} %copy-done, f32[2,256,128]{2,1,0:T(8,128)} %whole.1) | non-fusion elementwise | flops 65536 | bytes 786432 | tf_op jit(solution)/shard_map/add | solution.py:453
Async XLA Ops:
  0.0 33.4 %copy-start = (f32[2,256,128]{2,1,0:T(8,128)S(1)}, f32[2,256,128]{2,1,0:T(8,128)}, u32[]{:S(2)}) copy-start(f32[2,256,128]{2,1,0:T(8,128)} %ens_in.1) | copy-start | bytes 786436
where the time goes:
time: 35.2 us; the launch traced here: 35.1 us
  Pallas kernels  33.4 us (95%)
  other arithmetic  1.68 us (5%)
    pallas_call x1, Pallas kernels, by_rows(): pl.pallas_call(functools.partial(whole_kernel, n), out_shape=jax.ShapeDty...  33.4 us
    add x1, other arithmetic, by_rows(): return ensemble + z  1.68 us

commit v1 on v0

v1 whole, which is shorter than its diff:
```python
import functools
import math

import jax
import jax.numpy as jnp
from jax import lax
from jax.experimental import pallas as pl
from jax.experimental.pallas import tpu as pltpu
from jax.sharding import PartitionSpec as P

REACH = 16
ITERS = 3


def from_behind(value, axis, steps):
    count = lax.axis_size(axis)
    first, last = (max(0, -steps), min(count, count - steps))
    return lax.ppermute(value, axis, [(source, source + steps) for source in range(first, last)])


def small_solve(gram, target):
    size = gram.shape[0]
    factor = {}
    for block_position in range(size):
        running = gram[block_position, block_position]
        for k in range(block_position):
            running = running - factor[block_position, k] * factor[block_position, k]
        factor[block_position, block_position] = jnp.sqrt(running)
        for i in range(block_position + 1, size):
            running = gram[i, block_position]
            for k in range(block_position):
                running = running - factor[i, k] * factor[block_position, k]
            factor[i, block_position] = running / factor[block_position, block_position]
    forward = []
    for i in range(size):
        running = target[i]
        for k in range(i):
            running = running - factor[i, k] * forward[k]
        forward.append(running / factor[i, i])
    analysis_output = [None] * size
    for i in reversed(range(size)):
        running = forward[i]
        for k in range(i + 1, size):
            running = running - factor[k, i] * analysis_output[k]
        analysis_output[i] = running / factor[i, i]
    return jnp.stack(analysis_output)


def previous_blocks(entry_values, reach_devices):
    pieces = [
        from_behind(entry_values, ("region", "blk"), shift_by)
        for shift_by in range(reach_devices, 0, -1)
    ]
    return jnp.concatenate(pieces, axis=0)


def on_device(ensemble, observed, obs_var, ridge, pred_back, bounds):
    highest = lax.Precision.HIGHEST
    local_blocks, rows, members = ensemble.shape
    slots = pred_back.shape[1]
    reach_devices = -(-REACH // local_blocks)
    before = reach_devices * local_blocks
    anomaly = (ensemble - jnp.mean(ensemble, axis=2, keepdims=True)) / jnp.sqrt(
        jnp.float32(members - 1)
    )
    positions = before + jnp.arange(local_blocks, dtype=jnp.int32)[:, None] - pred_back
    positions = jnp.where(pred_back > 0, positions, before + local_blocks)
    empty_zero_matrix = jnp.zeros((1, rows, members), jnp.float32)

    def extend(entry_values):
        return jnp.concatenate(
            [previous_blocks(entry_values, reach_devices), entry_values, empty_zero_matrix], axis=0
        )

    preds = extend(anomaly)[positions]
    identity = jnp.eye(slots, dtype=jnp.float32)
    gram = jnp.einsum("bjrm,bkrm->jkbr", preds, preds, precision=highest)
    gram = gram + ridge[None, None, :, None] * identity[:, :, None, None]
    target = jnp.einsum("bjrm,brm->jbr", preds, anomaly, precision=highest)
    regression_coefficients = small_solve(gram, target)
    resid = anomaly - jnp.einsum("jbr,bjrm->brm", regression_coefficients, preds, precision=highest)
    inverse_var = 1.0 / (jnp.sum(resid * resid, axis=2) + 1e-05)
    inverse_obs = 1.0 / obs_var
    beta_blocks = jnp.transpose(regression_coefficients, (1, 0, 2))
    lower_bound = bounds[0]
    upper_bound = bounds[1]
    theta = (upper_bound + lower_bound) / 2
    delta = (upper_bound - lower_bound) / 2
    sigma = theta / delta
    rho_now = 1.0 / sigma
    residue = inverse_obs[:, :, None] * (observed - ensemble)
    increment = jnp.zeros_like(ensemble)
    direction = residue / theta
    for step in range(ITERS):
        increment = increment + direction
        extended = extend(direction)
        lower_analysis_output = direction
        for lower_slot in range(slots):
            lower_analysis_output = (
                lower_analysis_output
                - beta_blocks[:, lower_slot, :, None] * extended[positions[:, lower_slot]]
            )
        upper_entry_values = lower_analysis_output * inverse_var[:, :, None]
        window = jnp.zeros((before + local_blocks + 1, rows, members), jnp.float32)
        for slot in range(slots):
            window = window.at[positions[:, slot]].add(
                beta_blocks[:, slot, :, None] * upper_entry_values
            )
        analysis_output = upper_entry_values - window[before : before + local_blocks]
        for shift_by in range(1, reach_devices + 1):
            start = (reach_devices - shift_by) * local_blocks
            analysis_output = analysis_output - from_behind(
                window[start : start + local_blocks], ("region", "blk"), -shift_by
            )
        residue = residue - (analysis_output + inverse_obs[:, :, None] * direction)
        rho_next = 1.0 / (2 * sigma - rho_now)
        direction = rho_next * rho_now * direction + 2 * rho_next / delta * residue
        rho_now = rho_next
    increment = increment + direction
    return ensemble + increment


VMEM_GRANT = 66_700_000
SUB = 8
HALF = SUB // 2
LANES = 128
MESH_ID = pl.DeviceIdType.MESH
HIGHEST = lax.Precision.HIGHEST


def place():
    per = lax.axis_size("blk")
    region, blk = lax.axis_index("region"), lax.axis_index("blk")
    return lax.axis_size("region"), per, region, blk, region * per + blk


def each_peer(where, visit):
    regions, per, region, blk, unused = where
    half = per // 2
    mine = blk // half

    def on(base):
        def step(i, carry):
            to = lax.rem(region + lax.rem(i, regions), regions)
            at = base + lax.rem(blk + i // regions, half)
            visit((to, at), to * per + at)
            return carry

        return step

    lax.fori_loop(0, regions * half, on((1 - mine) * half), 0)
    lax.fori_loop(1, regions * half, on(mine * half), 0)


def copy_to(src, dst, send_sem, recv_sem, device):
    return pltpu.make_async_remote_copy(
        src_ref=src,
        dst_ref=dst,
        send_sem=send_sem,
        recv_sem=recv_sem,
        device_id=device,
        device_id_type=MESH_ID,
    )


def tile_at(k):
    return pl.ds(pl.multiple_of(k * SUB, SUB), SUB)


def swap(x):
    return pltpu.roll(x, HALF, 0)


def pair_rows(n, src, dst):
    low = lax.broadcasted_iota(jnp.int32, (SUB, LANES), 0) < HALF
    for k in range(n):
        at = slice(k * SUB, (k + 1) * SUB)
        first, second = src[0, at, :], src[1, at, :]
        dst[0, at, :] = jnp.where(low, first, swap(second))
        dst[1, at, :] = jnp.where(low, swap(first), second)


def fill_pack(rows, obs_var, ridge, pred_back, pack):
    local = pred_back.shape[0]
    lane = lax.broadcasted_iota(jnp.int32, (1, LANES), 1)
    groups = LANES // SUB
    for block in range(local):
        meta = jnp.where(lane == SUB + REACH, ridge[block], 0.0)
        for slot in range(pred_back.shape[1]):
            back = pred_back[block, slot]
            meta = jnp.where((lane == back + (SUB - 1)) & (lane >= SUB), 1.0, meta)
        for part in range(rows // LANES):
            row = obs_var[block : block + 1, part * LANES : (part + 1) * LANES]
            for k in range(groups):
                turned = row if k == 0 else pltpu.roll(row, LANES - SUB * k, 1)
                pack[part * groups + k, block] = jnp.where(lane < SUB, turned, meta)


def whole_kernel(
    n, bounds_in, ens_in, obs_in, obs_var_in, ridge_in, pred_back_in, z,
    bounds, ens, obs, obs_var, ridge, pred_back, load_sem,
    pack, ens_s, obs_s, ens_r, obs_r, pack_r, z_s, z_r, send_sem, recv_sem,
    anom, corr, filt,
):
    where = place()
    me = where[-1]
    local, rows, members = ens.shape
    loads = [
        pltpu.make_async_copy(src, dst, load_sem.at[i])
        for i, (src, dst) in enumerate(
            (
                (ens_in, ens),
                (obs_in, obs),
                (obs_var_in, obs_var),
                (ridge_in, ridge),
                (pred_back_in, pred_back),
                (bounds_in, bounds),
            )
        )
    ]
    for load in loads:
        load.start()
    barrier = pltpu.get_barrier_semaphore()

    def signal(device, k):
        pl.semaphore_signal(barrier, inc=1, device_id=device, device_id_type=MESH_ID)

    each_peer(where, signal)
    for load in loads:
        load.wait()
    own = tile_at(me)
    pair_rows(n, ens, ens_s)
    pair_rows(n, obs, obs_s)
    fill_pack(rows, obs_var, ridge, pred_back, pack)
    mine = pl.ds(me * local, local)
    ens_r[:, own, :] = ens_s[:, own, :]
    obs_r[:, own, :] = obs_s[:, own, :]
    pack_r[mine] = pack[me]
    pl.semaphore_wait(barrier, n - 1)

    def send_ens(device, k):
        copy_to(
            ens_s.at[:, tile_at(k), :], ens_r.at[:, own, :], send_sem.at[0], recv_sem.at[0], device
        ).start()

    def send_pack(device, k):
        copy_to(pack.at[k], pack_r.at[mine], send_sem.at[1], recv_sem.at[1], device).start()

    def send_half(src, dst, h, which):
        def send(device, k):
            copy_to(
                src.at[h, tile_at(k), :], dst.at[h, own, :], send_sem.at[which], recv_sem.at[which],
                device,
            ).start()

        return send

    each_peer(where, send_ens)
    each_peer(where, send_pack)
    each_peer(where, send_half(obs_s, obs_r, 0, 2))
    each_peer(where, send_half(obs_s, obs_r, 1, 3))

    others = pl.ds(0, (n - 1) * SUB)
    whole = (
        ens_r.at[:, others, :],
        pack_r.at[pl.ds(0, (n - 1) * local)],
        obs_r.at[0, others, :],
        obs_r.at[1, others, :],
        z_r.at[0, others, :],
        z_r.at[1, others, :],
    )
    regions, per, region, blk, unused = where
    neighbour = (lax.rem(region + 1, regions), blk)

    def arrived(which):
        ref = whole[which]
        copy_to(ref, ref, send_sem.at[which], recv_sem.at[which], neighbour).wait_recv()

    arrived(0)
    make_filters(n * local, arrived, bounds, ens_r, pack_r, anom, corr, filt)
    nb = n * local
    empty = jnp.zeros((LANES - nb, members), jnp.float32)
    for h in range(2):
        arrived(2 + h)
        for r in range(HALF):
            at = pl.ds(r, nb, stride=HALF)
            gap = obs_r[h, at, :] - ens_r[h, at, :]
            gap = jnp.concatenate([gap, empty] if h == 0 else [empty, gap], axis=0)
            z_s[h, at, :] = dot(filt[r, h * nb : (h + 1) * nb, :], gap, 1, 0)
        each_peer(where, send_half(z_s, z_r, h, 4 + h))
        z_r[h, own, :] = z_s[h, own, :]
    low = lax.broadcasted_iota(jnp.int32, (SUB, LANES), 0) < HALF
    arrived(4)
    arrived(5)
    for k in range(n):
        at = slice(k * SUB, (k + 1) * SUB)
        first, second = z_r[0, at, :], z_r[1, at, :]
        z[0, at, :] = jnp.where(low, first, swap(second))
        z[1, at, :] = jnp.where(low, swap(first), second)
    for which, ref in enumerate(whole):
        copy_to(ref, ref, send_sem.at[which], recv_sem.at[which], neighbour).wait_send()


def dot(lhs, rhs, left, right):
    return lax.dot_general(
        lhs,
        rhs,
        (((left,), (right,)), ((), ())),
        precision=HIGHEST,
        preferred_element_type=jnp.float32,
    )


def make_filters(nb, arrived, bounds, ens, pack, anom, corr, filt):
    members = ens.shape[2]
    square = (LANES, LANES)
    tile = (SUB, LANES)
    back = lax.broadcasted_iota(jnp.int32, square, 1) - lax.broadcasted_iota(jnp.int32, square, 0)
    corr[...] = jnp.zeros(corr.shape, jnp.float32)
    for r in range(HALF):
        at = pl.ds(r, nb, stride=HALF)
        x = jnp.concatenate([ens[0, at, :], ens[1, at, :]], axis=0)
        mean = jnp.sum(x, axis=1, keepdims=True) * (1.0 / members)
        x = (x - mean) * (1.0 / math.sqrt(members - 1))
        anom[r] = x
        full = dot(x, x, 1, 1)
        for delta in range(REACH + 1):
            corr[delta, r : r + 1, :] = jnp.sum(
                jnp.where(back == delta, full, 0.0), axis=0, keepdims=True
            )

    arrived(1)
    flat = pack[...].reshape(nb, LANES)
    turned = jnp.concatenate([flat, flat], axis=0).T
    on_lane = lax.broadcasted_iota(jnp.int32, tile, 1)
    obs_rows = jnp.where(on_lane < nb, turned[0:SUB], swap(turned[0:SUB]))
    inverse_obs = 1.0 / obs_rows
    chosen = [
        jnp.broadcast_to(turned[SUB + d : SUB + d + 1], tile) > 0.5 for d in range(REACH)
    ]
    at = SUB + REACH
    ridge = jnp.broadcast_to(turned[at : at + 1], tile)

    factor = {}
    inverse = []
    for j in range(REACH):
        for i in range(j, REACH):
            value = pltpu.roll(corr[i - j], j + 1, 1)
            running = jnp.where(chosen[j], jnp.where(chosen[i], value, 0.0), 0.0)
            if i == j:
                running = running + ridge
            for k in range(j):
                running = running - factor[i, k] * factor[j, k]
            if i == j:
                inverse.append(1.0 / jnp.sqrt(running))
            else:
                factor[i, j] = running * inverse[j]
    forward = []
    for i in range(REACH):
        running = jnp.where(chosen[i], corr[i + 1], 0.0)
        for k in range(i):
            running = running - factor[i, k] * forward[k]
        forward.append(running * inverse[i])
    beta = [None] * REACH
    for i in reversed(range(REACH)):
        running = forward[i]
        for k in range(i + 1, REACH):
            running = running - factor[k, i] * beta[k]
        beta[i] = running * inverse[i]

    lo = jnp.full((1, LANES), bounds[0], jnp.float32)
    hi = jnp.full((1, LANES), bounds[1], jnp.float32)
    theta = (hi + lo) / 2
    delta = (hi - lo) / 2
    sigma = theta / delta
    identity = jnp.where(back == 0, 1.0, 0.0)
    for r in range(HALF):
        upper = identity
        for d in range(REACH):
            upper = jnp.where(back == d + 1, -beta[d][r : r + 1], upper)
        resid = dot(anom[r], upper, 0, 0)
        inverse_var = 1.0 / (jnp.sum(resid * resid, axis=0, keepdims=True) + 1e-05)
        inverse_row = inverse_obs[r : r + 1]
        operator = dot(upper * inverse_var, upper, 1, 1) + jnp.where(back == 0, inverse_row, 0.0)
        rho = 1.0 / sigma
        direction = identity / theta
        total = direction
        residue = identity
        for step in range(ITERS):
            moved = operator / theta if step == 0 else dot(operator, direction, 1, 0)
            residue = residue - moved
            rho_next = 1.0 / (2 * sigma - rho)
            direction = rho_next * rho * direction + 2 * rho_next / delta * residue
            rho = rho_next
            total = total + direction
        filt[r] = total * inverse_row


def by_rows(n, ensemble, observed, obs_var, ridge, pred_back, bounds):
    local, rows, members = ensemble.shape
    nb = n * local
    f32 = jnp.float32
    vmem = pl.BlockSpec(memory_space=pltpu.VMEM)
    hbm = pl.BlockSpec(memory_space=pltpu.HBM)
    halves = pltpu.VMEM((2, n * SUB, members), f32)
    z = pl.pallas_call(
        functools.partial(whole_kernel, n),
        out_shape=jax.ShapeDtypeStruct(ensemble.shape, f32),
        in_specs=[hbm] * 6,
        out_specs=vmem,
        scratch_shapes=[
            pltpu.SMEM(bounds.shape, f32),
            pltpu.VMEM(ensemble.shape, f32),
            pltpu.VMEM(observed.shape, f32),
            pltpu.VMEM(obs_var.shape, f32),
            pltpu.SMEM(ridge.shape, f32),
            pltpu.SMEM(pred_back.shape, jnp.int32),
            pltpu.SemaphoreType.DMA((6,)),
            pltpu.VMEM((n, local, 1, LANES), f32),
            halves,
            halves,
            halves,
            halves,
            pltpu.VMEM((nb, 1, LANES), f32),
            halves,
            halves,
            pltpu.SemaphoreType.DMA((6,)),
            pltpu.SemaphoreType.DMA((6,)),
            pltpu.VMEM((HALF, LANES, LANES), f32),
            pltpu.VMEM((REACH + 1, SUB, LANES), f32),
            pltpu.VMEM((HALF, LANES, LANES), f32),
        ],
        compiler_params=pltpu.CompilerParams(
            collective_id=0, has_side_effects=True, vmem_limit_bytes=VMEM_GRANT
        ),
        name="whole",
    )(bounds, ensemble, observed, obs_var, ridge, pred_back)
    return ensemble + z


def choose(n, ensemble, *rest):
    local, rows, members = ensemble.shape
    even = lax.axis_size("blk") % 2 == 0 and local == 2
    if even and rows == n * SUB and members == LANES and 2 * n * local == LANES:
        return by_rows(n, ensemble, *rest)
    return on_device(ensemble, *rest)


def solution(mesh):
    return jax.shard_map(
        functools.partial(choose, mesh.size),
        mesh=mesh,
        in_specs=(
            P(("region", "blk"), None, None),
            P(("region", "blk"), None, None),
            P(("region", "blk"), None),
            P(("region", "blk")),
            P(("region", "blk"), None),
            P(),
        ),
        out_specs=P(("region", "blk"), None, None),
        check_vma=False,
    )
```

time: 35.2 us -> 35.1 us (level)
  no operation moved by 1% of the time
where the time goes in v1:
time: 35.1 us; the launch traced here: 34.9 us
  Pallas kernels  33.2 us (95%)
  other arithmetic  1.68 us (5%)
    pallas_call x1, Pallas kernels, by_rows(): pl.pallas_call(functools.partial(whole_kernel, n), out_shape=jax.ShapeDty...  33.2 us
    add x1, other arithmetic, by_rows(): return ensemble + z  1.68 us

profile of v1, /device:TPU:0, one launch (start us, length us, event | category | flops | bytes accessed | tf_op | source)
XLA Modules:
  0.0 34.9 jit_solution(17422132666750405811)
XLA Ops:
  0.0 0.0 copy-start
  0.0 33.2 %whole.1 = f32[2,256,128]{2,1,0:T(8,128)} custom-call(f32[2]{0:T(128)} %bounds_in.1, f32[2,256,128]{2,1,0:T(8,128)} %ens_in.1, f32[2,256,128]{2,1,0:T(8,128)} %obs_in.1, f32[2,256]{1,0:T(2,128)} %obs_var_in.1, f32[2]{0:T(128)} %ridge_in.1, s32[2,12]{1,0:T(2,128)} %pred_back_in.1), custom_call_target="tpu_custom_call" | custom-call | tf_op jit(solution)/shard_map/whole/pallas_call | solution.py:406
  33.2 0.0 copy-done
  33.2 1.7 %add.3 = f32[2,256,128]{2,1,0:T(8,128)} add(f32[2,256,128]{2,1,0:T(8,128)S(1)} %copy-done, f32[2,256,128]{2,1,0:T(8,128)} %whole.1) | non-fusion elementwise | flops 65536 | bytes 786432 | tf_op jit(solution)/shard_map/add | solution.py:438
Async XLA Ops:
  0.0 33.2 %copy-start = (f32[2,256,128]{2,1,0:T(8,128)S(1)}, f32[2,256,128]{2,1,0:T(8,128)}, u32[]{:S(2)}) copy-start(f32[2,256,128]{2,1,0:T(8,128)} %ens_in.1) | copy-start | bytes 786436

commit v2 on v1

--- a/solution.py
+++ b/solution.py
@@ -135,21 +135,13 @@
 
 
 def each_peer(where, visit):
-    regions, per, region, blk, unused = where
-    half = per // 2
-    mine = blk // half
-
-    def on(base):
-        def step(i, carry):
-            to = lax.rem(region + lax.rem(i, regions), regions)
-            at = base + lax.rem(blk + i // regions, half)
-            visit((to, at), to * per + at)
-            return carry
-
-        return step
-
-    lax.fori_loop(0, regions * half, on((1 - mine) * half), 0)
-    lax.fori_loop(1, regions * half, on(mine * half), 0)
+    regions, per, region, blk, me = where
+    n = regions * per
+    def step(i, carry):
+        k = lax.rem(me + i, n)
+        visit((k // per, lax.rem(k, per)), k)
+        return carry
+    lax.fori_loop(1, n, step, 0)
 
 
 def copy_to(src, dst, send_sem, recv_sem, device):
@@ -199,8 +191,8 @@
 def whole_kernel(
     n, bounds_in, ens_in, obs_in, obs_var_in, ridge_in, pred_back_in, z,
     bounds, ens, obs, obs_var, ridge, pred_back, load_sem,
-    pack, ens_s, obs_s, ens_r, obs_r, pack_r, z_s, z_r, send_sem, recv_sem,
-    anom, corr, filt,
+    pack, obs_s, ens_r, obs_r, pack_r, z_s, z_r, send_sem, recv_sem,
+    corr, filt,
 ):
     where = place()
     me = where[-1]
@@ -226,21 +218,14 @@
         pl.semaphore_signal(barrier, inc=1, device_id=device, device_id_type=MESH_ID)
 
     each_peer(where, signal)
-    for load in loads:
-        load.wait()
     own = tile_at(me)
-    pair_rows(n, ens, ens_s)
-    pair_rows(n, obs, obs_s)
-    fill_pack(rows, obs_var, ridge, pred_back, pack)
     mine = pl.ds(me * local, local)
-    ens_r[:, own, :] = ens_s[:, own, :]
-    obs_r[:, own, :] = obs_s[:, own, :]
-    pack_r[mine] = pack[me]
+    loads[0].wait()
     pl.semaphore_wait(barrier, n - 1)
 
     def send_ens(device, k):
         copy_to(
-            ens_s.at[:, tile_at(k), :], ens_r.at[:, own, :], send_sem.at[0], recv_sem.at[0], device
+            ens.at[:, tile_at(k), :], ens_r.at[mine], send_sem.at[0], recv_sem.at[0], device
         ).start()
 
     def send_pack(device, k):
@@ -256,13 +241,20 @@
         return send
 
     each_peer(where, send_ens)
+    for load in loads[1:]:
+        load.wait()
+    fill_pack(rows, obs_var, ridge, pred_back, pack)
     each_peer(where, send_pack)
+    pair_rows(n, obs, obs_s)
     each_peer(where, send_half(obs_s, obs_r, 0, 2))
     each_peer(where, send_half(obs_s, obs_r, 1, 3))
 
+    ens_r[mine] = ens[:, own, :]
+    pack_r[mine] = pack[me]
+    obs_r[:, own, :] = obs_s[:, own, :]
     others = pl.ds(0, (n - 1) * SUB)
     whole = (
-        ens_r.at[:, others, :],
+        ens_r.at[pl.ds(0, (n - 1) * local)],
         pack_r.at[pl.ds(0, (n - 1) * local)],
         obs_r.at[0, others, :],
         obs_r.at[1, others, :],
@@ -277,16 +269,26 @@
         copy_to(ref, ref, send_sem.at[which], recv_sem.at[which], neighbour).wait_recv()
 
     arrived(0)
-    make_filters(n * local, arrived, bounds, ens_r, pack_r, anom, corr, filt)
+    make_filters(n * local, arrived, bounds, ens_r, pack_r, corr, filt)
     nb = n * local
-    empty = jnp.zeros((LANES - nb, members), jnp.float32)
+    empty = jnp.zeros((nb, members), jnp.float32)
     for h in range(2):
         arrived(2 + h)
-        for r in range(HALF):
-            at = pl.ds(r, nb, stride=HALF)
-            gap = obs_r[h, at, :] - ens_r[h, at, :]
-            gap = jnp.concatenate([gap, empty] if h == 0 else [empty, gap], axis=0)
-            z_s[h, at, :] = dot(filt[r, h * nb : (h + 1) * nb, :], gap, 1, 0)
+        for pair in range(HALF // 2):
+            gaps = [
+                obs_r[h, pl.ds(r, nb, stride=HALF), :] - ens_r[pl.ds(0, nb), h * HALF + r, :]
+                for r in (2 * pair, 2 * pair + 1)
+            ]
+            columns = []
+            for r in range(2):
+                column = [empty] * 4
+                column[2 * r + h] = gaps[r]
+                columns.append(jnp.concatenate(column, axis=0))
+            found = dot(filt[pair], jnp.concatenate(columns, axis=1), 1, 0)
+            for r in range(2):
+                z_s[h, pl.ds(2 * pair + r, nb, stride=HALF), :] = found[
+                    :, r * members : (r + 1) * members
+                ]
         each_peer(where, send_half(z_s, z_r, h, 4 + h))
         z_r[h, own, :] = z_s[h, own, :]
     low = lax.broadcasted_iota(jnp.int32, (SUB, LANES), 0) < HALF
@@ -311,19 +313,38 @@
     )
 
 
-def make_filters(nb, arrived, bounds, ens, pack, anom, corr, filt):
+def spread(x, on):
+    return jnp.where(on, jnp.concatenate([x] * (x.shape[1] // x.shape[0]), axis=0), 0.0)
+
+
+def make_filters(nb, arrived, bounds, ens, pack, corr, filt):
     members = ens.shape[2]
-    square = (LANES, LANES)
     tile = (SUB, LANES)
-    back = lax.broadcasted_iota(jnp.int32, square, 1) - lax.broadcasted_iota(jnp.int32, square, 0)
+    wide = 2 * LANES
+    back = lax.rem(lax.broadcasted_iota(jnp.int32, (nb, LANES), 1), nb) - lax.broadcasted_iota(
+        jnp.int32, (nb, LANES), 0
+    )
+    on = lax.broadcasted_iota(jnp.int32, (wide, wide), 0) // nb == lax.broadcasted_iota(
+        jnp.int32, (wide, wide), 1
+    ) // nb
+    empty = jnp.zeros((nb, members), jnp.float32)
     corr[...] = jnp.zeros(corr.shape, jnp.float32)
+    anom = []
     for r in range(HALF):
-        at = pl.ds(r, nb, stride=HALF)
-        x = jnp.concatenate([ens[0, at, :], ens[1, at, :]], axis=0)
-        mean = jnp.sum(x, axis=1, keepdims=True) * (1.0 / members)
-        x = (x - mean) * (1.0 / math.sqrt(members - 1))
-        anom[r] = x
-        full = dot(x, x, 1, 1)
+        sides = []
+        for h in range(2):
+            x = ens[pl.ds(0, nb), h * HALF + r, :]
+            mean = jnp.sum(x, axis=1, keepdims=True) * (1.0 / members)
+            sides.append((x - mean) * (1.0 / math.sqrt(members - 1)))
+        anom.append(jnp.concatenate(sides, axis=0))
+        rhs = jnp.concatenate(
+            [
+                jnp.concatenate([sides[0], empty], axis=1),
+                jnp.concatenate([empty, sides[1]], axis=1),
+            ],
+            axis=0,
+        )
+        full = dot(jnp.concatenate(sides, axis=1), rhs, 1, 1)
         for delta in range(REACH + 1):
             corr[delta, r : r + 1, :] = jnp.sum(
                 jnp.where(back == delta, full, 0.0), axis=0, keepdims=True
@@ -368,32 +389,57 @@
             running = running - factor[k, i] * beta[k]
         beta[i] = running * inverse[i]
 
-    lo = jnp.full((1, LANES), bounds[0], jnp.float32)
-    hi = jnp.full((1, LANES), bounds[1], jnp.float32)
+    lo = jnp.full((1, wide), bounds[0], jnp.float32)
+    hi = jnp.full((1, wide), bounds[1], jnp.float32)
     theta = (hi + lo) / 2
     delta = (hi - lo) / 2
     sigma = theta / delta
-    identity = jnp.where(back == 0, 1.0, 0.0)
-    for r in range(HALF):
-        upper = identity
-        for d in range(REACH):
-            upper = jnp.where(back == d + 1, -beta[d][r : r + 1], upper)
-        resid = dot(anom[r], upper, 0, 0)
-        inverse_var = 1.0 / (jnp.sum(resid * resid, axis=0, keepdims=True) + 1e-05)
-        inverse_row = inverse_obs[r : r + 1]
-        operator = dot(upper * inverse_var, upper, 1, 1) + jnp.where(back == 0, inverse_row, 0.0)
-        rho = 1.0 / sigma
-        direction = identity / theta
-        total = direction
-        residue = identity
-        for step in range(ITERS):
-            moved = operator / theta if step == 0 else dot(operator, direction, 1, 0)
-            residue = residue - moved
-            rho_next = 1.0 / (2 * sigma - rho)
-            direction = rho_next * rho * direction + 2 * rho_next / delta * residue
-            rho = rho_next
-            total = total + direction
-        filt[r] = total * inverse_row
+    here = back == 0
+    identity = jnp.where(jnp.concatenate([here, here], axis=1), 1.0, 0.0)
+    pairs = range(HALF // 2)
+    rows = lambda pair: (2 * pair, 2 * pair + 1)
+    inverse_row = [
+        jnp.concatenate([inverse_obs[r : r + 1] for r in rows(pair)], axis=1) for pair in pairs
+    ]
+    upper = []
+    for pair in pairs:
+        sides = []
+        for r in rows(pair):
+            side = jnp.where(here, 1.0, 0.0)
+            for d in range(REACH):
+                side = jnp.where(back == d + 1, -beta[d][r : r + 1], side)
+            sides.append(side)
+        upper.append(jnp.concatenate(sides, axis=1))
+    spread_upper = [spread(x, on) for x in upper]
+    resid = [
+        dot(jnp.concatenate([anom[r] for r in rows(pair)], axis=0), spread_upper[pair], 0, 0)
+        for pair in pairs
+    ]
+    inverse_var = [1.0 / (jnp.sum(x * x, axis=0, keepdims=True) + 1e-05) for x in resid]
+    operator = [
+        dot(upper[pair] * inverse_var[pair], spread_upper[pair], 1, 1)
+        + identity * inverse_row[pair]
+        for pair in pairs
+    ]
+    spread_operator = [spread(x, on) for x in operator]
+    rho = 1.0 / sigma
+    direction = [identity / theta for pair in pairs]
+    total = direction
+    residue = [identity for pair in pairs]
+    for step in range(ITERS):
+        moved = [
+            operator[pair] / theta if step == 0 else dot(direction[pair], spread_operator[pair], 1, 0)
+            for pair in pairs
+        ]
+        residue = [residue[pair] - moved[pair] for pair in pairs]
+        rho_next = 1.0 / (2 * sigma - rho)
+        keep = rho_next * rho
+        move = 2 * rho_next / delta
+        rho = rho_next
+        direction = [keep * direction[pair] + move * residue[pair] for pair in pairs]
+        total = [total[pair] + direction[pair] for pair in pairs]
+    for pair in pairs:
+        filt[pair] = total[pair] * inverse_row[pair]
 
 
 def by_rows(n, ensemble, observed, obs_var, ridge, pred_back, bounds):
@@ -418,17 +464,15 @@
             pltpu.SemaphoreType.DMA((6,)),
             pltpu.VMEM((n, local, 1, LANES), f32),
             halves,
-            halves,
-            halves,
+            pltpu.VMEM((nb, SUB, members), f32),
             halves,
             pltpu.VMEM((nb, 1, LANES), f32),
             halves,
             halves,
             pltpu.SemaphoreType.DMA((6,)),
             pltpu.SemaphoreType.DMA((6,)),
-            pltpu.VMEM((HALF, LANES, LANES), f32),
             pltpu.VMEM((REACH + 1, SUB, LANES), f32),
-            pltpu.VMEM((HALF, LANES, LANES), f32),
+            pltpu.VMEM((HALF // 2, nb, 2 * LANES), f32),
         ],
         compiler_params=pltpu.CompilerParams(
             collective_id=0, has_side_effects=True, vmem_limit_bytes=VMEM_GRANT

time: 35.1 us -> 32 us (0.912)
  Pallas kernels: 33.2 us -> 30.1 us
    pallas_call x1, Pallas kernels: 33.2 us -> 30.1 us  [by_rows(): pl.pallas_call(functools.partial(whole_kernel, n), out_shape=jax.ShapeDty...]
where the time goes in v2:
time: 32 us; the launch traced here: 31.8 us
  Pallas kernels  30.1 us (94%)
  other arithmetic  1.68 us (5%)
    pallas_call x1, Pallas kernels, by_rows(): pl.pallas_call(functools.partial(whole_kernel, n), out_shape=jax.ShapeDty...  30.1 us
    add x1, other arithmetic, by_rows(): return ensemble + z  1.68 us

profile of v2, /device:TPU:0, one launch (start us, length us, event | category | flops | bytes accessed | tf_op | source)
XLA Modules:
  0.0 31.8 jit_solution(6710129086933066109)
XLA Ops:
  0.0 0.0 copy-start
  0.0 30.1 %whole.1 = f32[2,256,128]{2,1,0:T(8,128)} custom-call(f32[2]{0:T(128)} %bounds_in.1, f32[2,256,128]{2,1,0:T(8,128)} %ens_in.1, f32[2,256,128]{2,1,0:T(8,128)} %obs_in.1, f32[2,256]{1,0:T(2,128)} %obs_var_in.1, f32[2]{0:T(128)} %ridge_in.1, s32[2,12]{1,0:T(2,128)} %pred_back_in.1), custom_call_target="tpu_custom_call" | custom-call | tf_op jit(solution)/shard_map/whole/pallas_call | solution.py:452
  30.1 0.0 copy-done
  30.2 1.7 %add.3 = f32[2,256,128]{2,1,0:T(8,128)} add(f32[2,256,128]{2,1,0:T(8,128)S(1)} %copy-done, f32[2,256,128]{2,1,0:T(8,128)} %whole.1) | non-fusion elementwise | flops 65536 | bytes 786432 | tf_op jit(solution)/shard_map/add | solution.py:482
Async XLA Ops:
  0.0 30.1 %copy-start = (f32[2,256,128]{2,1,0:T(8,128)S(1)}, f32[2,256,128]{2,1,0:T(8,128)}, u32[]{:S(2)}) copy-start(f32[2,256,128]{2,1,0:T(8,128)} %ens_in.1) | copy-start | bytes 786436

commit v3 on v2

--- a/solution.py
+++ b/solution.py
@@ -120,10 +120,11 @@
     return ensemble + increment
 
 
-VMEM_GRANT = 66_700_000
+VMEM_GRANT = 48_000_000
 SUB = 8
 HALF = SUB // 2
 LANES = 128
+PLANES = 4
 MESH_ID = pl.DeviceIdType.MESH
 HIGHEST = lax.Precision.HIGHEST
 
@@ -134,14 +135,25 @@
     return lax.axis_size("region"), per, region, blk, region * per + blk
 
 
-def each_peer(where, visit):
-    regions, per, region, blk, me = where
-    n = regions * per
-    def step(i, carry):
-        k = lax.rem(me + i, n)
-        visit((k // per, lax.rem(k, per)), k)
-        return carry
-    lax.fori_loop(1, n, step, 0)
+def peer(where, up, j):
+    regions, per, region, blk, unused = where
+    depth = per // PLANES
+    plane = lax.rem(blk // depth + up, PLANES)
+    at = lax.rem(region * depth + lax.rem(blk, depth) + j, regions * depth)
+    to, blk_to = at // depth, plane * depth + lax.rem(at, depth)
+    return (to, blk_to), to * per + blk_to
+
+
+def each_peer(where, visit, before=lambda up: None):
+    width = where[0] * where[1] // PLANES
+    for up in range(PLANES):
+        before(up)
+
+        def step(j, carry, up=up):
+            visit(*peer(where, up, j))
+            return carry
+
+        lax.fori_loop(0 if up else 1, width, step, 0)
 
 
 def copy_to(src, dst, send_sem, recv_sem, device):
@@ -191,7 +203,7 @@
 def whole_kernel(
     n, bounds_in, ens_in, obs_in, obs_var_in, ridge_in, pred_back_in, z,
     bounds, ens, obs, obs_var, ridge, pred_back, load_sem,
-    pack, obs_s, ens_r, obs_r, pack_r, z_s, z_r, send_sem, recv_sem,
+    pack, obs_s, ens_r, obs_r, pack_r, z_s, z_r, ready, send_sem, recv_sem,
     corr, filt,
 ):
     where = place()
@@ -214,14 +226,26 @@
         load.start()
     barrier = pltpu.get_barrier_semaphore()
 
-    def signal(device, k):
-        pl.semaphore_signal(barrier, inc=1, device_id=device, device_id_type=MESH_ID)
-
-    each_peer(where, signal)
+
+    def signal(sem, up, j):
+        device, unused = peer(where, up, j)
+        pl.semaphore_signal(sem, inc=1, device_id=device, device_id_type=MESH_ID)
+
+    width = n // PLANES
+    for up in range(1, PLANES):
+        signal(barrier, up, 0)
+    for j in range(1, width):
+        signal(barrier, 0, j)
     own = tile_at(me)
     mine = pl.ds(me * local, local)
+    pl.semaphore_wait(barrier, width - 1 + PLANES - 1)
+    for up in range(1, PLANES):
+        signal(ready.at[PLANES - up], up, 0)
     loads[0].wait()
-    pl.semaphore_wait(barrier, n - 1)
+
+    def plane_ready(up):
+        if up:
+            pl.semaphore_wait(ready.at[up], 1)
 
     def send_ens(device, k):
         copy_to(
@@ -240,7 +264,7 @@
 
         return send
 
-    each_peer(where, send_ens)
+    each_peer(where, send_ens, plane_ready)
     for load in loads[1:]:
         load.wait()
     fill_pack(rows, obs_var, ridge, pred_back, pack)
@@ -451,7 +475,7 @@
     halves = pltpu.VMEM((2, n * SUB, members), f32)
     z = pl.pallas_call(
         functools.partial(whole_kernel, n),
-        out_shape=jax.ShapeDtypeStruct(ensemble.shape, f32),
+        out_shape=pltpu.VMEM(ensemble.shape, f32),
         in_specs=[hbm] * 6,
         out_specs=vmem,
         scratch_shapes=[
@@ -469,6 +493,7 @@
             pltpu.VMEM((nb, 1, LANES), f32),
             halves,
             halves,
+            pltpu.SemaphoreType.REGULAR((PLANES,)),
             pltpu.SemaphoreType.DMA((6,)),
             pltpu.SemaphoreType.DMA((6,)),
             pltpu.VMEM((REACH + 1, SUB, LANES), f32),
@@ -478,13 +503,16 @@
             collective_id=0, has_side_effects=True, vmem_limit_bytes=VMEM_GRANT
         ),
         name="whole",
-    )(bounds, ensemble, observed, obs_var, ridge, pred_back)
+    )(*[
+        pltpu.with_memory_space_constraint(x, pltpu.HBM)
+        for x in (bounds, ensemble, observed, obs_var, ridge, pred_back)
+    ])
     return ensemble + z
 
 
 def choose(n, ensemble, *rest):
     local, rows, members = ensemble.shape
-    even = lax.axis_size("blk") % 2 == 0 and local == 2
+    even = lax.axis_size("blk") % PLANES == 0 and local == 2
     if even and rows == n * SUB and members == LANES and 2 * n * local == LANES:
         return by_rows(n, ensemble, *rest)
     return on_device(ensemble, *rest)

time: 32 us -> 30.6 us (0.956)
  other arithmetic: 1.68 us -> 0.73 us
  Pallas kernels: 30.1 us -> 29.7 us
    add x1, other arithmetic: 1.68 us -> 0.73 us  [by_rows(): return ensemble + z]
    pallas_call x1, Pallas kernels: 30.1 us -> 29.7 us  [by_rows(): pl.pallas_call(functools.partial(whole_kernel, n), out_shape=pltpu.VMEM(e...]
where the time goes in v3:
time: 30.6 us; the launch traced here: 30.4 us
  Pallas kernels  29.7 us (97%)
  other arithmetic  0.73 us (2%)
    pallas_call x1, Pallas kernels, by_rows(): pl.pallas_call(functools.partial(whole_kernel, n), out_shape=pltpu.VMEM(e...  29.7 us
    add x1, other arithmetic, by_rows(): return ensemble + z  0.73 us

profile of v3, /device:TPU:0, one launch (start us, length us, event | category | flops | bytes accessed | tf_op | source)
XLA Modules:
  0.0 30.4 jit_solution(3539578101340399851)
XLA Ops:
  0.0 0.0 copy-start
  0.0 29.7 %whole.1 = f32[2,256,128]{2,1,0:T(8,128)S(1)} custom-call(f32[2]{0:T(128)} %bounds_in.1, f32[2,256,128]{2,1,0:T(8,128)} %ens_in.1, f32[2,256,128]{2,1,0:T(8,128)} %obs_in.1, f32[2,256]{1,0:T(2,128)} %obs_var_in.1, f32[2]{0:T(128)} %ridge_in.1, s32[2,12]{1,0:T(2,128)} %pred_back_in.1), custom_call_target="tpu_custom_call" | custom-call | tf_op jit(solution)/shard_map/whole/pallas_call | solution.py:476
  29.7 0.0 copy-done
  29.7 0.7 %add.3 = f32[2,256,128]{2,1,0:T(8,128)} add(f32[2,256,128]{2,1,0:T(8,128)S(1)} %copy-done, f32[2,256,128]{2,1,0:T(8,128)S(1)} %whole.1) | non-fusion elementwise | flops 65536 | bytes 786432 | tf_op jit(solution)/shard_map/add | solution.py:510
Async XLA Ops:
  0.0 29.7 %copy-start = (f32[2,256,128]{2,1,0:T(8,128)S(1)}, f32[2,256,128]{2,1,0:T(8,128)}, u32[]{:S(2)}) copy-start(f32[2,256,128]{2,1,0:T(8,128)} %ens_in.1) | copy-start | bytes 786436

commit v4 on v3

--- a/solution.py
+++ b/solution.py
@@ -188,6 +188,7 @@
     local = pred_back.shape[0]
     lane = lax.broadcasted_iota(jnp.int32, (1, LANES), 1)
     groups = LANES // SUB
+    side = LANES // local
     for block in range(local):
         meta = jnp.where(lane == SUB + REACH, ridge[block], 0.0)
         for slot in range(pred_back.shape[1]):
@@ -197,13 +198,17 @@
             row = obs_var[block : block + 1, part * LANES : (part + 1) * LANES]
             for k in range(groups):
                 turned = row if k == 0 else pltpu.roll(row, LANES - SUB * k, 1)
-                pack[part * groups + k, block] = jnp.where(lane < SUB, turned, meta)
+                turned = jnp.where(lane < SUB, turned, meta)
+                at = part * groups + k
+                if block:
+                    turned = jnp.where(lane < side, pack[at], pltpu.roll(turned, side, 1))
+                pack[at] = turned
 
 
 def whole_kernel(
     n, bounds_in, ens_in, obs_in, obs_var_in, ridge_in, pred_back_in, z,
     bounds, ens, obs, obs_var, ridge, pred_back, load_sem,
-    pack, obs_s, ens_r, obs_r, pack_r, z_s, z_r, ready, send_sem, recv_sem,
+    pack, obs_s, ens_r, obs_r, pack_r, facts, z_s, z_r, ready, send_sem, recv_sem,
     corr, filt,
 ):
     where = place()
@@ -232,20 +237,16 @@
         pl.semaphore_signal(sem, inc=1, device_id=device, device_id_type=MESH_ID)
 
     width = n // PLANES
-    for up in range(1, PLANES):
-        signal(barrier, up, 0)
-    for j in range(1, width):
-        signal(barrier, 0, j)
+    for up in range(PLANES):
+        for j in range(0 if up else 1, width): signal(barrier, up, j)
     own = tile_at(me)
     mine = pl.ds(me * local, local)
-    pl.semaphore_wait(barrier, width - 1 + PLANES - 1)
-    for up in range(1, PLANES):
-        signal(ready.at[PLANES - up], up, 0)
+    pl.semaphore_wait(barrier, n - 1)
     loads[0].wait()
 
     def plane_ready(up):
         if up:
-            pl.semaphore_wait(ready.at[up], 1)
+            pass
 
     def send_ens(device, k):
         copy_to(
@@ -253,7 +254,7 @@
         ).start()
 
     def send_pack(device, k):
-        copy_to(pack.at[k], pack_r.at[mine], send_sem.at[1], recv_sem.at[1], device).start()
+        copy_to(pack.at[k], pack_r.at[me], send_sem.at[1], recv_sem.at[1], device).start()
 
     def send_half(src, dst, h, which):
         def send(device, k):
@@ -274,12 +275,12 @@
     each_peer(where, send_half(obs_s, obs_r, 1, 3))
 
     ens_r[mine] = ens[:, own, :]
-    pack_r[mine] = pack[me]
+    pack_r[me] = pack[me]
     obs_r[:, own, :] = obs_s[:, own, :]
     others = pl.ds(0, (n - 1) * SUB)
     whole = (
         ens_r.at[pl.ds(0, (n - 1) * local)],
-        pack_r.at[pl.ds(0, (n - 1) * local)],
+        pack_r.at[pl.ds(0, n - 1)],
         obs_r.at[0, others, :],
         obs_r.at[1, others, :],
         z_r.at[0, others, :],
@@ -293,7 +294,7 @@
         copy_to(ref, ref, send_sem.at[which], recv_sem.at[which], neighbour).wait_recv()
 
     arrived(0)
-    make_filters(n * local, arrived, bounds, ens_r, pack_r, corr, filt)
+    make_filters(n * local, arrived, bounds, ens_r, pack_r, facts, corr, filt)
     nb = n * local
     empty = jnp.zeros((nb, members), jnp.float32)
     for h in range(2):
@@ -308,7 +309,7 @@
                 column = [empty] * 4
                 column[2 * r + h] = gaps[r]
                 columns.append(jnp.concatenate(column, axis=0))
-            found = dot(filt[pair], jnp.concatenate(columns, axis=1), 1, 0)
+            found = dot_split(filt[pair], jnp.concatenate(columns, axis=1), 0)
             for r in range(2):
                 z_s[h, pl.ds(2 * pair + r, nb, stride=HALF), :] = found[
                     :, r * members : (r + 1) * members
@@ -337,11 +338,27 @@
     )
 
 
+def halves_of(x):
+    high = x.astype(jnp.bfloat16)
+    return high, (x - high.astype(jnp.float32)).astype(jnp.bfloat16)
+
+
+def dot_split(lhs, rhs, right):
+    product = lambda a, b: lax.dot_general(
+        a, b, (((1,), (right,)), ((), ())), preferred_element_type=jnp.float32
+    )
+    rows = lhs.shape[0]
+    left_high, left_low = halves_of(lhs)
+    right_high, right_low = halves_of(rhs)
+    both = product(jnp.concatenate([left_high, left_low], axis=0), right_high)
+    return both[:rows] + (both[rows:] + product(left_high, right_low))
+
+
 def spread(x, on):
     return jnp.where(on, jnp.concatenate([x] * (x.shape[1] // x.shape[0]), axis=0), 0.0)
 
 
-def make_filters(nb, arrived, bounds, ens, pack, corr, filt):
+def make_filters(nb, arrived, bounds, ens, pack, facts, corr, filt):
     members = ens.shape[2]
     tile = (SUB, LANES)
     wide = 2 * LANES
@@ -375,7 +392,13 @@
             )
 
     arrived(1)
-    flat = pack[...].reshape(nb, LANES)
+    devices = pack.shape[0]
+    local = nb // devices
+    flat = pack[...].reshape(devices, LANES)
+    for block in range(local):
+        turned = pltpu.roll(flat, block * (LANES // local), 1) if block else flat
+        facts[pl.ds(block, devices, stride=local), :] = turned
+    flat = facts[...]
     turned = jnp.concatenate([flat, flat], axis=0).T
     on_lane = lax.broadcasted_iota(jnp.int32, tile, 1)
     obs_rows = jnp.where(on_lane < nb, turned[0:SUB], swap(turned[0:SUB]))
@@ -397,7 +420,7 @@
             for k in range(j):
                 running = running - factor[i, k] * factor[j, k]
             if i == j:
-                inverse.append(1.0 / jnp.sqrt(running))
+                inverse.append(lax.rsqrt(running))
             else:
                 factor[i, j] = running * inverse[j]
     forward = []
@@ -441,7 +464,7 @@
     ]
     inverse_var = [1.0 / (jnp.sum(x * x, axis=0, keepdims=True) + 1e-05) for x in resid]
     operator = [
-        dot(upper[pair] * inverse_var[pair], spread_upper[pair], 1, 1)
+        dot_split(upper[pair] * inverse_var[pair], spread_upper[pair], 1)
         + identity * inverse_row[pair]
         for pair in pairs
     ]
@@ -452,7 +475,7 @@
     residue = [identity for pair in pairs]
     for step in range(ITERS):
         moved = [
-            operator[pair] / theta if step == 0 else dot(direction[pair], spread_operator[pair], 1, 0)
+            operator[pair] / theta if step == 0 else dot_split(direction[pair], spread_operator[pair], 0)
             for pair in pairs
         ]
         residue = [residue[pair] - moved[pair] for pair in pairs]
@@ -486,11 +509,12 @@
             pltpu.SMEM(ridge.shape, f32),
             pltpu.SMEM(pred_back.shape, jnp.int32),
             pltpu.SemaphoreType.DMA((6,)),
-            pltpu.VMEM((n, local, 1, LANES), f32),
+            pltpu.VMEM((n, 1, LANES), f32),
             halves,
             pltpu.VMEM((nb, SUB, members), f32),
             halves,
-            pltpu.VMEM((nb, 1, LANES), f32),
+            pltpu.VMEM((n, 1, LANES), f32),
+            pltpu.VMEM((nb, LANES), f32),
             halves,
             halves,
             pltpu.SemaphoreType.REGULAR((PLANES,)),

time: 30.6 us -> 29 us (0.948)
  Pallas kernels: 29.7 us -> 28.2 us
    pallas_call x1, Pallas kernels: 29.7 us -> 28.2 us  [by_rows(): pl.pallas_call(functools.partial(whole_kernel, n), out_shape=pltpu.VMEM(e...]
where the time goes in v4:
time: 29 us; the launch traced here: 28.9 us
  Pallas kernels  28.2 us (97%)
  other arithmetic  0.73 us (3%)
    pallas_call x1, Pallas kernels, by_rows(): pl.pallas_call(functools.partial(whole_kernel, n), out_shape=pltpu.VMEM(e...  28.2 us
    add x1, other arithmetic, by_rows(): return ensemble + z  0.73 us

profile of v4, /device:TPU:0, one launch (start us, length us, event | category | flops | bytes accessed | tf_op | source)
XLA Modules:
  0.0 28.9 jit_solution(17647337510708304150)
XLA Ops:
  0.0 0.0 copy-start
  0.0 28.2 %whole.1 = f32[2,256,128]{2,1,0:T(8,128)S(1)} custom-call(f32[2]{0:T(128)} %bounds_in.1, f32[2,256,128]{2,1,0:T(8,128)} %ens_in.1, f32[2,256,128]{2,1,0:T(8,128)} %obs_in.1, f32[2,256]{1,0:T(2,128)} %obs_var_in.1, f32[2]{0:T(128)} %ridge_in.1, s32[2,12]{1,0:T(2,128)} %pred_back_in.1), custom_call_target="tpu_custom_call" | custom-call | tf_op jit(solution)/shard_map/whole/pallas_call | solution.py:499
  28.2 0.0 copy-done
  28.2 0.7 %add.3 = f32[2,256,128]{2,1,0:T(8,128)} add(f32[2,256,128]{2,1,0:T(8,128)S(1)} %copy-done, f32[2,256,128]{2,1,0:T(8,128)S(1)} %whole.1) | non-fusion elementwise | flops 65536 | bytes 786432 | tf_op jit(solution)/shard_map/add | solution.py:534
Async XLA Ops:
  0.0 28.2 %copy-start = (f32[2,256,128]{2,1,0:T(8,128)S(1)}, f32[2,256,128]{2,1,0:T(8,128)}, u32[]{:S(2)}) copy-start(f32[2,256,128]{2,1,0:T(8,128)} %ens_in.1) | copy-start | bytes 786436

commit v5 on v4

--- a/solution.py
+++ b/solution.py
@@ -125,6 +125,8 @@
 HALF = SUB // 2
 LANES = 128
 PLANES = 4
+PARTS = 1
+PART = SUB // PARTS
 MESH_ID = pl.DeviceIdType.MESH
 HIGHEST = lax.Precision.HIGHEST
 
@@ -146,8 +148,7 @@
 
 def each_peer(where, visit, before=lambda up: None):
     width = where[0] * where[1] // PLANES
-    for up in range(PLANES):
-        before(up)
+    for up in [1, 2, 3, 0]:
 
         def step(j, carry, up=up):
             visit(*peer(where, up, j))
@@ -167,28 +168,22 @@
     )
 
 
+def part_at(part):
+    return pl.ds(part * PART, PART)
+
+
+def rows_at(k, part):
+    return pl.ds(pl.multiple_of(k * SUB + part * PART, PART), PART)
+
+
 def tile_at(k):
     return pl.ds(pl.multiple_of(k * SUB, SUB), SUB)
 
 
-def swap(x):
-    return pltpu.roll(x, HALF, 0)
-
-
-def pair_rows(n, src, dst):
-    low = lax.broadcasted_iota(jnp.int32, (SUB, LANES), 0) < HALF
-    for k in range(n):
-        at = slice(k * SUB, (k + 1) * SUB)
-        first, second = src[0, at, :], src[1, at, :]
-        dst[0, at, :] = jnp.where(low, first, swap(second))
-        dst[1, at, :] = jnp.where(low, swap(first), second)
-
-
-def fill_pack(rows, obs_var, ridge, pred_back, pack):
+def fill_facts(rows, obs_var, ridge, pred_back, ens_s):
     local = pred_back.shape[0]
     lane = lax.broadcasted_iota(jnp.int32, (1, LANES), 1)
     groups = LANES // SUB
-    side = LANES // local
     for block in range(local):
         meta = jnp.where(lane == SUB + REACH, ridge[block], 0.0)
         for slot in range(pred_back.shape[1]):
@@ -198,27 +193,25 @@
             row = obs_var[block : block + 1, part * LANES : (part + 1) * LANES]
             for k in range(groups):
                 turned = row if k == 0 else pltpu.roll(row, LANES - SUB * k, 1)
-                turned = jnp.where(lane < SUB, turned, meta)
-                at = part * groups + k
-                if block:
-                    turned = jnp.where(lane < side, pack[at], pltpu.roll(turned, side, 1))
-                pack[at] = turned
+                ens_s[block, part * groups + k, SUB : SUB + 1, :] = jnp.where(
+                    lane < SUB, turned, meta
+                )
 
 
 def whole_kernel(
     n, bounds_in, ens_in, obs_in, obs_var_in, ridge_in, pred_back_in, z,
-    bounds, ens, obs, obs_var, ridge, pred_back, load_sem,
-    pack, obs_s, ens_r, obs_r, pack_r, facts, z_s, z_r, ready, send_sem, recv_sem,
+    bounds, ens_s, obs, obs_var, ridge, pred_back, load_sem,
+    ens_r, obs_r, z_s, send_sem, recv_sem,
     corr, filt,
 ):
     where = place()
     me = where[-1]
-    local, rows, members = ens.shape
+    local, rows, members = obs.shape
     loads = [
         pltpu.make_async_copy(src, dst, load_sem.at[i])
         for i, (src, dst) in enumerate(
             (
-                (ens_in, ens),
+                (ens_in.reshape(local, n, SUB, members), ens_s.at[:, :, pl.ds(0, SUB), :]),
                 (obs_in, obs),
                 (obs_var_in, obs_var),
                 (ridge_in, ridge),
@@ -241,50 +234,46 @@
         for j in range(0 if up else 1, width): signal(barrier, up, j)
     own = tile_at(me)
     mine = pl.ds(me * local, local)
+    held = pl.ds(0, SUB + 1)
+    for load in loads:
+        load.wait()
+    fill_facts(rows, obs_var, ridge, pred_back, ens_s)
     pl.semaphore_wait(barrier, n - 1)
-    loads[0].wait()
-
-    def plane_ready(up):
-        if up:
-            pass
-
     def send_ens(device, k):
         copy_to(
-            ens.at[:, tile_at(k), :], ens_r.at[mine], send_sem.at[0], recv_sem.at[0], device
+            ens_s.at[:, k, held, :], ens_r.at[mine, held, :], send_sem.at[0], recv_sem.at[0], device
         ).start()
 
-    def send_pack(device, k):
-        copy_to(pack.at[k], pack_r.at[me], send_sem.at[1], recv_sem.at[1], device).start()
-
-    def send_half(src, dst, h, which):
+    def send_obs(part):
         def send(device, k):
             copy_to(
-                src.at[h, tile_at(k), :], dst.at[h, own, :], send_sem.at[which], recv_sem.at[which],
-                device,
+                obs.at[:, rows_at(k, part), :], obs_r.at[mine, part_at(part), :],
+                send_sem.at[1 + part], recv_sem.at[1 + part], device,
             ).start()
 
         return send
 
-    each_peer(where, send_ens, plane_ready)
-    for load in loads[1:]:
-        load.wait()
-    fill_pack(rows, obs_var, ridge, pred_back, pack)
-    each_peer(where, send_pack)
-    pair_rows(n, obs, obs_s)
-    each_peer(where, send_half(obs_s, obs_r, 0, 2))
-    each_peer(where, send_half(obs_s, obs_r, 1, 3))
-
-    ens_r[mine] = ens[:, own, :]
-    pack_r[me] = pack[me]
-    obs_r[:, own, :] = obs_s[:, own, :]
-    others = pl.ds(0, (n - 1) * SUB)
+    def send_z(part):
+        def send(device, k):
+            copy_to(
+                z_s.at[pl.ds(k * local, local), part_at(part), :], z.at[:, rows_at(me, part), :],
+                send_sem.at[1 + PARTS + part], recv_sem.at[1 + PARTS + part], device,
+            ).start()
+
+        return send
+
+    each_peer(where, send_ens)
+    for part in range(PARTS):
+        each_peer(where, send_obs(part))
+
+    ens_r[mine, held, :] = ens_s[:, me, held, :]
+    obs_r[mine] = obs[:, own, :]
+    got = pl.ds(0, (n - 1) * local)
+    sent = pl.ds(0, (n - 1) * SUB)
     whole = (
-        ens_r.at[pl.ds(0, (n - 1) * local)],
-        pack_r.at[pl.ds(0, n - 1)],
-        obs_r.at[0, others, :],
-        obs_r.at[1, others, :],
-        z_r.at[0, others, :],
-        z_r.at[1, others, :],
+        ens_r.at[got, held, :],
+        *[obs_r.at[got, part_at(part), :] for part in range(PARTS)],
+        *[z_s.at[got, part_at(part), :] for part in range(PARTS)],
     )
     regions, per, region, blk, unused = where
     neighbour = (lax.rem(region + 1, regions), blk)
@@ -294,36 +283,25 @@
         copy_to(ref, ref, send_sem.at[which], recv_sem.at[which], neighbour).wait_recv()
 
     arrived(0)
-    make_filters(n * local, arrived, bounds, ens_r, pack_r, facts, corr, filt)
+    make_filters(n * local, bounds, ens_r, corr, filt)
     nb = n * local
     empty = jnp.zeros((nb, members), jnp.float32)
-    for h in range(2):
-        arrived(2 + h)
-        for pair in range(HALF // 2):
-            gaps = [
-                obs_r[h, pl.ds(r, nb, stride=HALF), :] - ens_r[pl.ds(0, nb), h * HALF + r, :]
-                for r in (2 * pair, 2 * pair + 1)
-            ]
+    for part in range(PARTS):
+        arrived(1 + part)
+        for r in range(part * PART, (part + 1) * PART, 2):
+            h, pair = r // HALF, r % HALF // 2
             columns = []
-            for r in range(2):
+            for side in range(2):
                 column = [empty] * 4
-                column[2 * r + h] = gaps[r]
+                column[2 * side + h] = obs_r[:, r + side, :] - ens_r[:, r + side, :]
                 columns.append(jnp.concatenate(column, axis=0))
             found = dot_split(filt[pair], jnp.concatenate(columns, axis=1), 0)
-            for r in range(2):
-                z_s[h, pl.ds(2 * pair + r, nb, stride=HALF), :] = found[
-                    :, r * members : (r + 1) * members
-                ]
-        each_peer(where, send_half(z_s, z_r, h, 4 + h))
-        z_r[h, own, :] = z_s[h, own, :]
-    low = lax.broadcasted_iota(jnp.int32, (SUB, LANES), 0) < HALF
-    arrived(4)
-    arrived(5)
-    for k in range(n):
-        at = slice(k * SUB, (k + 1) * SUB)
-        first, second = z_r[0, at, :], z_r[1, at, :]
-        z[0, at, :] = jnp.where(low, first, swap(second))
-        z[1, at, :] = jnp.where(low, swap(first), second)
+            for side in range(2):
+                z_s[:, r + side, :] = found[:, side * members : (side + 1) * members]
+        each_peer(where, send_z(part))
+    z[:, own, :] = z_s[mine]
+    for part in range(PARTS):
+        arrived(1 + PARTS + part)
     for which, ref in enumerate(whole):
         copy_to(ref, ref, send_sem.at[which], recv_sem.at[which], neighbour).wait_send()
 
@@ -358,7 +336,7 @@
     return jnp.where(on, jnp.concatenate([x] * (x.shape[1] // x.shape[0]), axis=0), 0.0)
 
 
-def make_filters(nb, arrived, bounds, ens, pack, facts, corr, filt):
+def make_filters(nb, bounds, ens, corr, filt):
     members = ens.shape[2]
     tile = (SUB, LANES)
     wide = 2 * LANES
@@ -374,7 +352,7 @@
     for r in range(HALF):
         sides = []
         for h in range(2):
-            x = ens[pl.ds(0, nb), h * HALF + r, :]
+            x = ens[:, h * HALF + r, :]
             mean = jnp.sum(x, axis=1, keepdims=True) * (1.0 / members)
             sides.append((x - mean) * (1.0 / math.sqrt(members - 1)))
         anom.append(jnp.concatenate(sides, axis=0))
@@ -391,17 +369,10 @@
                 jnp.where(back == delta, full, 0.0), axis=0, keepdims=True
             )
 
-    arrived(1)
-    devices = pack.shape[0]
-    local = nb // devices
-    flat = pack[...].reshape(devices, LANES)
-    for block in range(local):
-        turned = pltpu.roll(flat, block * (LANES // local), 1) if block else flat
-        facts[pl.ds(block, devices, stride=local), :] = turned
-    flat = facts[...]
+    flat = ens[:, SUB, :]
     turned = jnp.concatenate([flat, flat], axis=0).T
     on_lane = lax.broadcasted_iota(jnp.int32, tile, 1)
-    obs_rows = jnp.where(on_lane < nb, turned[0:SUB], swap(turned[0:SUB]))
+    obs_rows = jnp.where(on_lane < nb, turned[0:SUB], pltpu.roll(turned[0:SUB], HALF, 0))
     inverse_obs = 1.0 / obs_rows
     chosen = [
         jnp.broadcast_to(turned[SUB + d : SUB + d + 1], tile) > 0.5 for d in range(REACH)
@@ -495,7 +466,7 @@
     f32 = jnp.float32
     vmem = pl.BlockSpec(memory_space=pltpu.VMEM)
     hbm = pl.BlockSpec(memory_space=pltpu.HBM)
-    halves = pltpu.VMEM((2, n * SUB, members), f32)
+    by_block = pltpu.VMEM((nb, SUB, members), f32)
     z = pl.pallas_call(
         functools.partial(whole_kernel, n),
         out_shape=pltpu.VMEM(ensemble.shape, f32),
@@ -503,23 +474,17 @@
         out_specs=vmem,
         scratch_shapes=[
             pltpu.SMEM(bounds.shape, f32),
-            pltpu.VMEM(ensemble.shape, f32),
+            pltpu.VMEM((local, n, 2 * SUB, members), f32),
             pltpu.VMEM(observed.shape, f32),
             pltpu.VMEM(obs_var.shape, f32),
             pltpu.SMEM(ridge.shape, f32),
             pltpu.SMEM(pred_back.shape, jnp.int32),
             pltpu.SemaphoreType.DMA((6,)),
-            pltpu.VMEM((n, 1, LANES), f32),
-            halves,
-            pltpu.VMEM((nb, SUB, members), f32),
-            halves,
-            pltpu.VMEM((n, 1, LANES), f32),
-            pltpu.VMEM((nb, LANES), f32),
-            halves,
-            halves,
-            pltpu.SemaphoreType.REGULAR((PLANES,)),
-            pltpu.SemaphoreType.DMA((6,)),
-            pltpu.SemaphoreType.DMA((6,)),
+            pltpu.VMEM((nb, 2 * SUB, members), f32),
+            by_block,
+            by_block,
+            pltpu.SemaphoreType.DMA((1 + 2 * PARTS,)),
+            pltpu.SemaphoreType.DMA((1 + 2 * PARTS,)),
             pltpu.VMEM((REACH + 1, SUB, LANES), f32),
             pltpu.VMEM((HALF // 2, nb, 2 * LANES), f32),
         ],

time: 29 us -> 29 us (level)
  no operation moved by 1% of the time
where the time goes in v5:
time: 29 us; the launch traced here: 28.8 us
  Pallas kernels  28.1 us (97%)
  other arithmetic  0.73 us (3%)
    pallas_call x1, Pallas kernels, by_rows(): pl.pallas_call(functools.partial(whole_kernel, n), out_shape=pltpu.VMEM(e...  28.1 us
    add x1, other arithmetic, by_rows(): return ensemble + z  0.73 us

profile of v5, /device:TPU:0, one launch (start us, length us, event | category | flops | bytes accessed | tf_op | source)
XLA Modules:
  0.0 28.8 jit_solution(715547515015767516)
XLA Ops:
  0.0 0.0 copy-start
  0.0 28.1 %whole.1 = f32[2,256,128]{2,1,0:T(8,128)S(1)} custom-call(f32[2]{0:T(128)} %bounds_in.1, f32[2,256,128]{2,1,0:T(8,128)} %ens_in.1, f32[2,256,128]{2,1,0:T(8,128)} %obs_in.1, f32[2,256]{1,0:T(2,128)} %obs_var_in.1, f32[2]{0:T(128)} %ridge_in.1, s32[2,12]{1,0:T(2,128)} %pred_back_in.1), custom_call_target="tpu_custom_call" | custom-call | tf_op jit(solution)/shard_map/whole/pallas_call | solution.py:470
  28.1 0.0 copy-done
  28.1 0.7 %add.3 = f32[2,256,128]{2,1,0:T(8,128)} add(f32[2,256,128]{2,1,0:T(8,128)S(1)} %copy-done, f32[2,256,128]{2,1,0:T(8,128)S(1)} %whole.1) | non-fusion elementwise | flops 65536 | bytes 786432 | tf_op jit(solution)/shard_map/add | solution.py:499
Async XLA Ops:
  0.0 28.1 %copy-start = (f32[2,256,128]{2,1,0:T(8,128)S(1)}, f32[2,256,128]{2,1,0:T(8,128)}, u32[]{:S(2)}) copy-start(f32[2,256,128]{2,1,0:T(8,128)} %ens_in.1) | copy-start | bytes 786436

commit v6 on v5

--- a/solution.py
+++ b/solution.py
@@ -126,6 +126,10 @@
 LANES = 128
 PLANES = 4
 PARTS = 1
+EARLY = 2
+SIGNALS = ((0, 1, 2, 3), (1, 2, 3, 0), (2, 3, 0, 1), (3, 0, 1, 2))
+ROUND = ((1, 2, 3, 0), (2, 3, 0, 1), (3, 0, 1, 2), (0, 1, 2, 3))
+BACK = ((1, 2, 3, 0), (2, 3, 0, 1), (0, 1, 3, 2), (0, 1, 2, 3))
 PART = SUB // PARTS
 MESH_ID = pl.DeviceIdType.MESH
 HIGHEST = lax.Precision.HIGHEST
@@ -137,24 +141,40 @@
     return lax.axis_size("region"), per, region, blk, region * per + blk
 
 
-def peer(where, up, j):
+def peer(where, plane, j):
     regions, per, region, blk, unused = where
     depth = per // PLANES
-    plane = lax.rem(blk // depth + up, PLANES)
     at = lax.rem(region * depth + lax.rem(blk, depth) + j, regions * depth)
-    to, blk_to = at // depth, plane * depth + lax.rem(at, depth)
-    return (to, blk_to), to * per + blk_to
-
-
-def each_peer(where, visit, before=lambda up: None):
-    width = where[0] * where[1] // PLANES
-    for up in [1, 2, 3, 0]:
-
-        def step(j, carry, up=up):
-            visit(*peer(where, up, j))
+    return at, (at // depth, plane * depth + lax.rem(at, depth))
+
+
+def each_peer(where, visit, order, early=0):
+    regions, per, region, blk, me = where
+    depth = per // PLANES
+    mine = blk // depth
+    for plane in range(PLANES):
+        for place in range(early):
+            k = plane * depth + place
+
+            @pl.when(me != k)
+            def ahead(k=k):
+                visit((jnp.int32(0), jnp.int32(k)), jnp.int32(k))
+
+    for turn in range(PLANES):
+        plane = order[-1][turn]
+        for z in range(PLANES - 1):
+            plane = jnp.where(mine == z, order[z][turn], plane)
+
+        def step(j, carry, plane=plane):
+            at, device = peer(where, plane, j)
+
+            @pl.when(at >= early)
+            def later():
+                visit(device, device[0] * per + device[1])
+
             return carry
 
-        lax.fori_loop(0 if up else 1, width, step, 0)
+        lax.fori_loop(jnp.where(plane == mine, 1, 0), regions * depth, step, 0)
 
 
 def copy_to(src, dst, send_sem, recv_sem, device):
@@ -225,13 +245,10 @@
     barrier = pltpu.get_barrier_semaphore()
 
 
-    def signal(sem, up, j):
-        device, unused = peer(where, up, j)
-        pl.semaphore_signal(sem, inc=1, device_id=device, device_id_type=MESH_ID)
-
-    width = n // PLANES
-    for up in range(PLANES):
-        for j in range(0 if up else 1, width): signal(barrier, up, j)
+    def signal(device, k):
+        pl.semaphore_signal(barrier, inc=1, device_id=device, device_id_type=MESH_ID)
+
+    each_peer(where, signal, SIGNALS, EARLY)
     own = tile_at(me)
     mine = pl.ds(me * local, local)
     held = pl.ds(0, SUB + 1)
@@ -239,6 +256,7 @@
         load.wait()
     fill_facts(rows, obs_var, ridge, pred_back, ens_s)
     pl.semaphore_wait(barrier, n - 1)
+
     def send_ens(device, k):
         copy_to(
             ens_s.at[:, k, held, :], ens_r.at[mine, held, :], send_sem.at[0], recv_sem.at[0], device
@@ -262,14 +280,12 @@
 
         return send
 
-    each_peer(where, send_ens)
+    each_peer(where, send_ens, ROUND)
     for part in range(PARTS):
-        each_peer(where, send_obs(part))
-
+        each_peer(where, send_obs(part), ROUND)
     ens_r[mine, held, :] = ens_s[:, me, held, :]
     obs_r[mine] = obs[:, own, :]
     got = pl.ds(0, (n - 1) * local)
-    sent = pl.ds(0, (n - 1) * SUB)
     whole = (
         ens_r.at[got, held, :],
         *[obs_r.at[got, part_at(part), :] for part in range(PARTS)],
@@ -298,7 +314,7 @@
             found = dot_split(filt[pair], jnp.concatenate(columns, axis=1), 0)
             for side in range(2):
                 z_s[:, r + side, :] = found[:, side * members : (side + 1) * members]
-        each_peer(where, send_z(part))
+        each_peer(where, send_z(part), BACK, EARLY)
     z[:, own, :] = z_s[mine]
     for part in range(PARTS):
         arrived(1 + PARTS + part)

time: 29 us -> 27.8 us (0.959)
  Pallas kernels: 28.1 us -> 26.9 us
    pallas_call x1, Pallas kernels: 28.1 us -> 26.9 us  [by_rows(): pl.pallas_call(functools.partial(whole_kernel, n), out_shape=pltpu.VMEM(e...]
where the time goes in v6:
time: 27.8 us; the launch traced here: 27.6 us
  Pallas kernels  26.9 us (97%)
  other arithmetic  0.73 us (3%)
    pallas_call x1, Pallas kernels, by_rows(): pl.pallas_call(functools.partial(whole_kernel, n), out_shape=pltpu.VMEM(e...  26.9 us
    add x1, other arithmetic, by_rows(): return ensemble + z  0.73 us

profile of v6, /device:TPU:0, one launch (start us, length us, event | category | flops | bytes accessed | tf_op | source)
XLA Modules:
  0.0 27.6 jit_solution(7613541405885715184)
XLA Ops:
  0.0 0.0 copy-start
  0.0 26.9 %whole.1 = f32[2,256,128]{2,1,0:T(8,128)S(1)} custom-call(f32[2]{0:T(128)} %bounds_in.1, f32[2,256,128]{2,1,0:T(8,128)} %ens_in.1, f32[2,256,128]{2,1,0:T(8,128)} %obs_in.1, f32[2,256]{1,0:T(2,128)} %obs_var_in.1, f32[2]{0:T(128)} %ridge_in.1, s32[2,12]{1,0:T(2,128)} %pred_back_in.1), custom_call_target="tpu_custom_call" | custom-call | tf_op jit(solution)/shard_map/whole/pallas_call | solution.py:486
  26.9 0.0 copy-done
  26.9 0.7 %add.3 = f32[2,256,128]{2,1,0:T(8,128)} add(f32[2,256,128]{2,1,0:T(8,128)S(1)} %copy-done, f32[2,256,128]{2,1,0:T(8,128)S(1)} %whole.1) | non-fusion elementwise | flops 65536 | bytes 786432 | tf_op jit(solution)/shard_map/add | solution.py:515
Async XLA Ops:
  0.0 26.9 %copy-start = (f32[2,256,128]{2,1,0:T(8,128)S(1)}, f32[2,256,128]{2,1,0:T(8,128)}, u32[]{:S(2)}) copy-start(f32[2,256,128]{2,1,0:T(8,128)} %ens_in.1) | copy-start | bytes 786436

commit v7 on v6

--- a/solution.py
+++ b/solution.py
@@ -341,11 +341,12 @@
     product = lambda a, b: lax.dot_general(
         a, b, (((1,), (right,)), ((), ())), preferred_element_type=jnp.float32
     )
-    rows = lhs.shape[0]
-    left_high, left_low = halves_of(lhs)
+    if lhs.dtype != jnp.bfloat16:
+        lhs = jnp.concatenate(halves_of(lhs), axis=0)
+    rows = lhs.shape[0] // 2
     right_high, right_low = halves_of(rhs)
-    both = product(jnp.concatenate([left_high, left_low], axis=0), right_high)
-    return both[:rows] + (both[rows:] + product(left_high, right_low))
+    both = product(lhs, right_high)
+    return both[:rows] + (both[rows:] + product(lhs[:rows], right_low))
 
 
 def spread(x, on):
@@ -473,7 +474,7 @@
         direction = [keep * direction[pair] + move * residue[pair] for pair in pairs]
         total = [total[pair] + direction[pair] for pair in pairs]
     for pair in pairs:
-        filt[pair] = total[pair] * inverse_row[pair]
+        filt[pair] = jnp.concatenate(halves_of(total[pair] * inverse_row[pair]), axis=0)
 
 
 def by_rows(n, ensemble, observed, obs_var, ridge, pred_back, bounds):
@@ -502,7 +503,7 @@
             pltpu.SemaphoreType.DMA((1 + 2 * PARTS,)),
             pltpu.SemaphoreType.DMA((1 + 2 * PARTS,)),
             pltpu.VMEM((REACH + 1, SUB, LANES), f32),
-            pltpu.VMEM((HALF // 2, nb, 2 * LANES), f32),
+            pltpu.VMEM((HALF // 2, 2 * nb, 2 * LANES), jnp.bfloat16),
         ],
         compiler_params=pltpu.CompilerParams(
             collective_id=0, has_side_effects=True, vmem_limit_bytes=VMEM_GRANT

time: 27.8 us -> 27.7 us (level)
  no operation moved by 1% of the time
where the time goes in v7:
time: 27.7 us; the launch traced here: 27.6 us
  Pallas kernels  26.9 us (97%)
  other arithmetic  0.73 us (3%)
    pallas_call x1, Pallas kernels, by_rows(): pl.pallas_call(functools.partial(whole_kernel, n), out_shape=pltpu.VMEM(e...  26.9 us
    add x1, other arithmetic, by_rows(): return ensemble + z  0.73 us

profile of v7, /device:TPU:0, one launch (start us, length us, event | category | flops | bytes accessed | tf_op | source)
XLA Modules:
  0.0 27.6 jit_solution(12410003900207163080)
XLA Ops:
  0.0 0.0 copy-start
  0.0 26.9 %whole.1 = f32[2,256,128]{2,1,0:T(8,128)S(1)} custom-call(f32[2]{0:T(128)} %bounds_in.1, f32[2,256,128]{2,1,0:T(8,128)} %ens_in.1, f32[2,256,128]{2,1,0:T(8,128)} %obs_in.1, f32[2,256]{1,0:T(2,128)} %obs_var_in.1, f32[2]{0:T(128)} %ridge_in.1, s32[2,12]{1,0:T(2,128)} %pred_back_in.1), custom_call_target="tpu_custom_call" | custom-call | tf_op jit(solution)/shard_map/whole/pallas_call | solution.py:487
  26.9 0.0 copy-done
  26.9 0.7 %add.3 = f32[2,256,128]{2,1,0:T(8,128)} add(f32[2,256,128]{2,1,0:T(8,128)S(1)} %copy-done, f32[2,256,128]{2,1,0:T(8,128)S(1)} %whole.1) | non-fusion elementwise | flops 65536 | bytes 786432 | tf_op jit(solution)/shard_map/add | solution.py:516
Async XLA Ops:
  0.0 26.9 %copy-start = (f32[2,256,128]{2,1,0:T(8,128)S(1)}, f32[2,256,128]{2,1,0:T(8,128)}, u32[]{:S(2)}) copy-start(f32[2,256,128]{2,1,0:T(8,128)} %ens_in.1) | copy-start | bytes 786436
